TPU v7x, 32 devices: a whole 2x2x4 slice. The times are simulated.
32 devices in a mesh: dp: 4 (over x, core), mp: 8 (over z, y).
Axes of the slice: x: 2, y: 2, z: 4, core: 2. Of those that a mesh axis runs over, the one named last changes fastest.
Arguments:
- tokens: bfloat16 [1280, 1792], P(('dp', 'mp')), may hold values from -6 to 6
- norm_gain: float32 [1792], replicated, may hold values from 0.5 to 1.5
- norm_bias: float32 [1792], replicated, may hold values from -3 to 3
- w_in: bfloat16 [1792, 15360], P('dp', 'mp'), may hold values from -0.125 to 0.125
- b_in: float32 [15360], P('mp'), may hold values from -3 to 3
- w_out: bfloat16 [15360, 1792], P('mp', 'dp'), may hold values from -0.046875 to 0.046875
- b_out: float32 [1792], replicated, may hold values from -3 to 3
Outputs:
- result: bfloat16 [1280, 1792], P(('dp', 'mp'))
All inputs are finite; a program needn't handle non-finite values.
Results may differ from a plain program's by a relative error of at most 0.0042.
Values may be sent and summed in bfloat16 or wider, within the bound.
A program may use at most 128 MiB of HBM per device.

v0:
```python
import jax
import jax.numpy as jnp
from jax import lax
from jax.sharding import PartitionSpec as P


def on_device(tokens, norm_gain, norm_bias, w_in, b_in, w_out, b_out):
    values = tokens.astype(jnp.float32)
    center = jnp.mean(values, axis=1, keepdims=True)
    spread = jnp.mean((values - center) ** 2, axis=1, keepdims=True)
    normed = ((values - center) / jnp.sqrt(spread + 1e-06) * norm_gain + norm_bias).astype(
        jnp.bfloat16
    )
    w_in_full = lax.all_gather(w_in, "dp", axis=0, tiled=True)
    gathered = lax.all_gather(normed, "mp", axis=0, tiled=True)
    pre = jnp.dot(gathered, w_in_full, preferred_element_type=jnp.float32) + b_in
    hidden = jax.nn.gelu(pre, approximate=False).astype(jnp.bfloat16)
    w_out_full = lax.all_gather(w_out, "dp", axis=1, tiled=True)
    summed = lax.psum_scatter(
        jnp.dot(hidden, w_out_full, preferred_element_type=jnp.float32),
        "mp",
        scatter_dimension=0,
        tiled=True,
    )
    return (values + summed + b_out).astype(jnp.bfloat16)


def solution(mesh):
    placed = (P(("dp", "mp"), None), P(), P(), P("dp", "mp"), P("mp"), P("mp", "dp"), P())
    return jax.shard_map(
        on_device, mesh=mesh, in_specs=placed, out_specs=P(("dp", "mp"), None), check_vma=False
    )
```

profile of v0, /device:TPU:0, one launch (start us, length us, event | category | flops | bytes accessed | tf_op | source)
XLA Modules:
  0.0 249.3 jit_solution(16586171305829466705)
XLA Ops:
  6.5 0.0 copy-start.2
  6.5 0.0 all-gather.4.cloned.1.call-start
  6.5 1.0 convert_reduce_fusion
  7.6 1.1 fusion.45
  8.7 1.7 fusion.48
  10.5 0.0 all-gather.4.cloned.1.call-update
  10.5 0.0 all-gather.6.cloned.1.call-start
  10.5 0.7 all-gather.6.cloned.1.call-update
  11.2 0.0 all-gather.8.cloned.1.call-start
  11.3 0.7 all-gather.8.cloned.1.call-update
  12.0 0.0 copy-start
  12.0 0.0 copy-start.1
  12.0 0.0 reduce-scatter.2.cloned.1.call-start
  12.0 42.5 %all-gather.4.cloned.1.call-done = bf16[320,1792]{1,0:T(8,128)(2,1)} async-done(((bf16[40,1792]{1,0:T(8,128)(2,1)}), bf16[320,1792]{1,0:T(8,128)(2,1)}) %all-gather.4.cloned.1.call-update) | async-done | bytes 1146896 | tf_op jit(solution)/shard_map/all_gather | solution.py:15
  54.6 49.7 %all-gather.6.cloned.1.call-done = bf16[1792,1920]{1,0:T(8,128)(2,1)} async-done(((bf16[448,1920]{1,0:T(8,128)(2,1)}), bf16[1792,1920]{1,0:T(8,128)(2,1)}) %all-gather.6.cloned.1.call-update) | async-done | bytes 6881296 | tf_op jit(solution)/shard_map/all_gather | solution.py:14
  104.3 51.3 %all-gather.8.cloned.1.call-done = bf16[1920,1792]{0,1:T(8,128)(2,1)} async-done(((bf16[1920,448]{0,1:T(8,128)(2,1)}), bf16[1920,1792]{0,1:T(8,128)(2,1)}) %all-gather.8.cloned.1.call-update) | async-done | bytes 6881296 | tf_op jit(solution)/shard_map/all_gather | solution.py:18
  155.6 0.0 copy-done.2
  155.6 15.7 %fusion.10 = f32[320,1792]{1,0:T(8,128)} fusion(bf16[1920,1792]{0,1:T(8,128)(2,1)} %all-gather.8.cloned.1.call-done, bf16[320,1792]{1,0:T(8,128)(2,1)} %all-gather.4.cloned.1.call-done, bf16[1792,1920]{1,0:T(8,128)(2,1)} %all-gather.6.cloned.1.call-done, f32[1920]{0:T(1024)S(1)} %copy-done.2), kind=kOutput, calls=%fused_computation.20 | convolution fusion | flops 4444569600 | bytes 17210880 | tf_op jit(solution)/shard_map/dot_general | solution.py:20
  171.3 0.0 reduce-scatter.2.cloned.1.call-update
  171.4 69.7 %reduce-scatter.2.cloned.1.call-done = f32[40,1792]{1,0:T(8,128)} async-done(((f32[320,1792]{1,0:T(8,128)}), f32[40,1792]{1,0:T(8,128)}) %reduce-scatter.2.cloned.1.call-update) | async-done | bytes 286736 | tf_op jit(solution)/shard_map/reduce_scatter | solution.py:19
  241.1 0.0 copy-done
  241.1 0.0 copy-done.1
  241.1 1.7 fusion.50
  (2 shorter events, 0.0 us)
Async XLA Ops:
  6.5 149.1 %copy-start.2 = (f32[1920]{0:T(1024)S(1)}, f32[1920]{0:T(1024)}, u32[]{:S(2)}) copy-start(f32[1920]{0:T(1024)} %param.11) | copy-start | bytes 23044
  6.5 48.0 %all-gather.4.cloned.1.call-start = ((), (), s32[]{:S(2)}) async-start(), calls=%async_computation.1 | async-start | bytes 1290240 | tf_op jit(solution)/shard_map/all_gather | solution.py:15
  10.5 93.8 %all-gather.6.cloned.1.call-start = ((), (), s32[]{:S(2)}) async-start(), calls=%async_computation.2 | async-start | bytes 8601600 | tf_op jit(solution)/shard_map/all_gather | solution.py:14
  11.2 144.4 %all-gather.8.cloned.1.call-start = ((), (), s32[]{:S(2)}) async-start(), calls=%async_computation.3 | async-start | bytes 8601600 | tf_op jit(solution)/shard_map/all_gather | solution.py:18
  12.0 229.1 %copy-start = (bf16[40,1792]{1,0:T(8,128)(2,1)S(1)}, bf16[40,1792]{1,0:T(8,128)(2,1)}, u32[]{:S(2)}) copy-start(bf16[40,1792]{1,0:T(8,128)(2,1)} %param.7) | copy-start | bytes 430084
  12.0 229.1 %copy-start.1 = (f32[1792]{0:T(1024)S(1)}, f32[1792]{0:T(1024)}, u32[]{:S(2)}) copy-start(f32[1792]{0:T(1024)} %param.13) | copy-start | bytes 21508
  12.0 229.1 %reduce-scatter.2.cloned.1.call-start = ((), (), s32[]{:S(2)}) async-start(), calls=%async_computation.4 | async-start | bytes 2580480 | tf_op jit(solution)/shard_map/reduce_scatter | solution.py:19
Sparse Core Ops, SparseCore 0:
  10.6 43.9 all-gather.3
  56.1 48.1 all-gather.5
  105.9 49.6 all-gather.7
  171.5 69.5 reduce-scatter.1
where the time goes:
time: 249 us
  waiting for transfers between devices  215 us (86%)
  matrix products  15.7 us (6%)
  between operations  13.2 us (5%)
  other arithmetic  5.56 us (2%)
    reduce_scatter x1, waiting for transfers between devices, on_device(): lax.psum_scatter(jnp.dot(hidden, w_out_full, preferred_element_type=jnp.f...  69.7 us
    all_gather x1, waiting for transfers between devices, on_device(): w_out_full = lax.all_gather(w_out, 'dp', axis=1, tiled=True)  51.3 us
    all_gather x1, waiting for transfers between devices, on_device(): w_in_full = lax.all_gather(w_in, 'dp', axis=0, tiled=True)  49.7 us
    all_gather x1, waiting for transfers between devices, on_device(): gathered = lax.all_gather(normed, 'mp', axis=0, tiled=True)  42.5 us
    dot_general x1, matrix products, on_device(): jnp.dot(hidden, w_out_full, preferred_element_type=jnp.float32)  15.7 us
  transfers between devices with their start and end apart: 4, of which 4 were waited for; matrix products, arithmetic and copies ran while one was open for 0% of the time, Pallas kernels for 0%

commit v1 on v0

--- a/solution.py
+++ b/solution.py
@@ -12,7 +12,14 @@
         jnp.bfloat16
     )
     w_in_full = lax.all_gather(w_in, "dp", axis=0, tiled=True)
-    gathered = lax.all_gather(normed, "mp", axis=0, tiled=True)
+    size = lax.axis_size("mp")
+    right = [(i, (i + 1) % size) for i in range(size)]
+    shards = [normed]
+    for far in range(1, size):
+        shards = [lax.ppermute(shards[0], "mp", right), *shards]
+    whole = jnp.concatenate(shards, axis=0)
+    shift = (lax.axis_index("mp") + 1) * shards[-1].shape[0]
+    gathered = jnp.roll(whole, shift, axis=0)
     pre = jnp.dot(gathered, w_in_full, preferred_element_type=jnp.float32) + b_in
     hidden = jax.nn.gelu(pre, approximate=False).astype(jnp.bfloat16)
     w_out_full = lax.all_gather(w_out, "dp", axis=1, tiled=True)

time: 249 us -> 206 us (0.83)
  waiting for transfers between devices: 215 us -> 172 us
  other arithmetic: 5.56 us -> 2.4 us
  starting transfers between devices: 0.12 us -> 3.14 us
    ppermute x0 -> x7, waiting for transfers between devices: none -> 54.8 us  [on_device(): shards = [lax.ppermute(shards[0], 'mp', right), *shards]]
    all_gather x1, waiting for transfers between devices: 49.7 us -> 0.02 us  [on_device(): w_in_full = lax.all_gather(w_in, 'dp', axis=0, tiled=True)]
    all_gather x1 -> x0, waiting for transfers between devices: 42.5 us -> none  [on_device(): gathered = lax.all_gather(normed, 'mp', axis=0, tiled=True)]
    all_gather x1, waiting for transfers between devices: 51.3 us -> 45.6 us  [on_device(): w_out_full = lax.all_gather(w_out, 'dp', axis=1, tiled=True)]
    ppermute x0 -> x7, starting transfers between devices: none -> 3.06 us  [on_device(): shards = [lax.ppermute(shards[0], 'mp', right), *shards]]
  transfers between devices with their start and end apart: 4 -> 10, of which waited for: 4 -> 9; matrix products, arithmetic and copies ran while one was open for 0% -> 0% of each run, Pallas kernels for 0% -> 0%
where the time goes in v1:
time: 206 us
  waiting for transfers between devices  172 us (83%)
  matrix products  15.4 us (7%)
  between operations  13.3 us (6%)
  starting transfers between devices  3.14 us (2%)
  other arithmetic  2.4 us (1%)
    reduce_scatter x1, waiting for transfers between devices, on_device(): lax.psum_scatter(jnp.dot(hidden, w_out_full, preferred_element_type=jnp.f...  69.8 us
    ppermute x7, waiting for transfers between devices, on_device(): shards = [lax.ppermute(shards[0], 'mp', right), *shards]  54.8 us
    all_gather x1, waiting for transfers between devices, on_device(): w_out_full = lax.all_gather(w_out, 'dp', axis=1, tiled=True)  45.6 us
    dot_general x1, matrix products, on_device(): jnp.dot(hidden, w_out_full, preferred_element_type=jnp.float32)  15.4 us
  transfers between devices with their start and end apart: 10, of which 9 were waited for; matrix products, arithmetic and copies ran while one was open for 0% of the time, Pallas kernels for 0%

profile of v1, /device:TPU:0, one launch (start us, length us, event | category | flops | bytes accessed | tf_op | source)
XLA Modules:
  0.0 206.1 jit_solution(7705632163236309295)
XLA Ops:
  6.5 0.7 all-gather.3.cloned.1.call-update
  7.3 0.0 all-gather.5.cloned.1.call-start
  7.3 0.7 all-gather.5.cloned.1.call-update
  8.0 0.0 reduce-scatter.2.cloned.1.call-start
  8.1 0.1 convert_reduce_fusion
  8.2 0.2 fusion.47
  8.4 0.0 copy-start.4
  8.5 0.1 fusion.50
  8.6 3.0 %collective-permute-start = (bf16[40,1792]{1,0:T(8,128)(2,1)S(1)}, bf16[40,1792]{1,0:T(8,128)(2,1)S(1)}, u32[]{:S(2)}, u32[]{:S(2)}) collective-permute-start(bf16[40,1792]{1,0:T(8,128)(2,1)S(1)} %fusion.50), channel_id=1, source_target_pairs={{0,1},{1,2},{2,3},{3,4},{4,5},{5,6},{6,7},{7,0},{8,9},{9,10},{10,1... | collective-permute-start | bytes 430088 | tf_op jit(solution)/shard_map/ppermute | solution.py:19
  11.6 6.8 %collective-permute-done = bf16[40,1792]{1,0:T(8,128)(2,1)S(1)} collective-permute-done((bf16[40,1792]{1,0:T(8,128)(2,1)S(1)}, bf16[40,1792]{1,0:T(8,128)(2,1)S(1)}, u32[]{:S(2)}, u32[]{:S(2)}) %collective-permute-start) | collective-permute-done | bytes 143392 | tf_op jit(solution)/shard_map/ppermute | solution.py:19
  18.4 7.8 %collective-permute-done.1 = bf16[40,1792]{1,0:T(8,128)(2,1)S(1)} collective-permute-done((bf16[40,1792]{1,0:T(8,128)(2,1)S(1)}, bf16[40,1792]{1,0:T(8,128)(2,1)S(1)}, u32[]{:S(2)}, u32[]{:S(2)}) %collective-permute-start.1) | collective-permute-done | bytes 143392 | tf_op jit(solution)/shard_map/ppermute | solution.py:19
  26.2 7.8 %collective-permute-done.2 = bf16[40,1792]{1,0:T(8,128)(2,1)S(1)} collective-permute-done((bf16[40,1792]{1,0:T(8,128)(2,1)S(1)}, bf16[40,1792]{1,0:T(8,128)(2,1)S(1)}, u32[]{:S(2)}, u32[]{:S(2)}) %collective-permute-start.2) | collective-permute-done | bytes 143392 | tf_op jit(solution)/shard_map/ppermute | solution.py:19
  34.0 7.8 %collective-permute-done.3 = bf16[40,1792]{1,0:T(8,128)(2,1)S(1)} collective-permute-done((bf16[40,1792]{1,0:T(8,128)(2,1)S(1)}, bf16[40,1792]{1,0:T(8,128)(2,1)S(1)}, u32[]{:S(2)}, u32[]{:S(2)}) %collective-permute-start.3) | collective-permute-done | bytes 143392 | tf_op jit(solution)/shard_map/ppermute | solution.py:19
  41.8 7.8 %collective-permute-done.4 = bf16[40,1792]{1,0:T(8,128)(2,1)S(1)} collective-permute-done((bf16[40,1792]{1,0:T(8,128)(2,1)S(1)}, bf16[40,1792]{1,0:T(8,128)(2,1)S(1)}, u32[]{:S(2)}, u32[]{:S(2)}) %collective-permute-start.4) | collective-permute-done | bytes 143392 | tf_op jit(solution)/shard_map/ppermute | solution.py:19
  49.7 9.0 %collective-permute-done.5 = bf16[40,1792]{1,0:T(8,128)(2,1)S(1)} collective-permute-done((bf16[40,1792]{1,0:T(8,128)(2,1)S(1)}, bf16[40,1792]{1,0:T(8,128)(2,1)S(1)}, u32[]{:S(2)}, u32[]{:S(2)}) %collective-permute-start.5) | collective-permute-done | bytes 143392 | tf_op jit(solution)/shard_map/ppermute | solution.py:19
  58.7 7.8 %collective-permute-done.6 = bf16[40,1792]{1,0:T(8,128)(2,1)S(1)} collective-permute-done((bf16[40,1792]{1,0:T(8,128)(2,1)S(1)}, bf16[40,1792]{1,0:T(8,128)(2,1)S(1)}, u32[]{:S(2)}, u32[]{:S(2)}) %collective-permute-start.6) | collective-permute-done | bytes 143392 | tf_op jit(solution)/shard_map/ppermute | solution.py:19
  66.6 0.1 constant_dynamic-update-slice_fusion.8
  66.9 0.1 constant_dynamic-update-slice_fusion
  67.0 0.0 all-gather.3.cloned.1.call-done
  67.0 45.6 %all-gather.5.cloned.1.call-done = bf16[1920,1792]{0,1:T(8,128)(2,1)} async-done(((bf16[1920,448]{0,1:T(8,128)(2,1)}), bf16[1920,1792]{0,1:T(8,128)(2,1)}) %all-gather.5.cloned.1.call-update) | async-done | bytes 6881296 | tf_op jit(solution)/shard_map/all_gather | solution.py:25
  112.7 15.4 %fusion.10 = f32[320,1792]{1,0:T(8,128)} fusion(bf16[1920,1792]{0,1:T(8,128)(2,1)} %all-gather.5.cloned.1.call-done, bf16[1792,1920]{1,0:T(8,128)(2,1)} %all-gather.3.cloned.1.call-done, f32[1920]{0:T(1024)S(1)} %copy-done.4, bf16[640,1792]{1,0:T(8,128)(2,1)S(1)} %constant_dynamic-update-slice_fusion, s32[]{:T(128)S(6)} %select_n.14), kind=kOutput, calls=%fused_computation.20 | convolution fusion | flops 4444569600 | bytes 17211396 | tf_op jit(solution)/shard_map/dot_general | solution.py:27
  128.1 0.0 reduce-scatter.2.cloned.1.call-update
  128.1 69.8 %reduce-scatter.2.cloned.1.call-done = f32[40,1792]{1,0:T(8,128)} async-done(((f32[320,1792]{1,0:T(8,128)}), f32[40,1792]{1,0:T(8,128)}) %reduce-scatter.2.cloned.1.call-update) | async-done | bytes 286736 | tf_op jit(solution)/shard_map/reduce_scatter | solution.py:26
  197.9 1.7 fusion.52
  (32 shorter events, 0.2 us)
Async XLA Ops:
  6.5 1.5 copy-start
  6.5 1.9 copy-start.2
  6.5 1.9 copy-start.1
  6.5 60.5 %all-gather.3.cloned.1.call-start = ((), (), s32[]{:S(2)}) async-start(), calls=%async_computation.1 | async-start | bytes 8601600 | tf_op jit(solution)/shard_map/all_gather | solution.py:14
  7.3 105.4 %all-gather.5.cloned.1.call-start = ((), (), s32[]{:S(2)}) async-start(), calls=%async_computation.2 | async-start | bytes 8601600 | tf_op jit(solution)/shard_map/all_gather | solution.py:25
  8.0 189.9 %reduce-scatter.2.cloned.1.call-start = ((), (), s32[]{:S(2)}) async-start(), calls=%async_computation.3 | async-start | bytes 2580480 | tf_op jit(solution)/shard_map/reduce_scatter | solution.py:26
  8.4 104.2 %copy-start.4 = (f32[1920]{0:T(1024)S(1)}, f32[1920]{0:T(1024)}, u32[]{:S(2)}) copy-start(f32[1920]{0:T(1024)} %param.11) | copy-start | bytes 23044
  8.6 9.8 %collective-permute-start = (bf16[40,1792]{1,0:T(8,128)(2,1)S(1)}, bf16[40,1792]{1,0:T(8,128)(2,1)S(1)}, u32[]{:S(2)}, u32[]{:S(2)}) collective-permute-start(bf16[40,1792]{1,0:T(8,128)(2,1)S(1)} %fusion.50), channel_id=1, source_target_pairs={{0,1},{1,2},{2,3},{3,4},{4,5},{5,6},{6,7},{7,0},{8,9},{9,10},{10,1... | collective-permute-start | bytes 430088 | tf_op jit(solution)/shard_map/ppermute | solution.py:19
  18.4 7.8 %collective-permute-start.1 = (bf16[40,1792]{1,0:T(8,128)(2,1)S(1)}, bf16[40,1792]{1,0:T(8,128)(2,1)S(1)}, u32[]{:S(2)}, u32[]{:S(2)}) collective-permute-start(bf16[40,1792]{1,0:T(8,128)(2,1)S(1)} %collective-permute-done), channel_id=1, source_target_pairs={{0,1},{1,2},{2,3},{3,4},{4,5},{5,6},{6,7},{7,0},{8,9},{9,10},{10,1... | collective-permute-start | bytes 430088 | tf_op jit(solution)/shard_map/ppermute | solution.py:19
  26.2 7.8 %collective-permute-start.2 = (bf16[40,1792]{1,0:T(8,128)(2,1)S(1)}, bf16[40,1792]{1,0:T(8,128)(2,1)S(1)}, u32[]{:S(2)}, u32[]{:S(2)}) collective-permute-start(bf16[40,1792]{1,0:T(8,128)(2,1)S(1)} %collective-permute-done.1), channel_id=1, source_target_pairs={{0,1},{1,2},{2,3},{3,4},{4,5},{5,6},{6,7},{7,0},{8,9},{9,10},{10,1... | collective-permute-start | bytes 430088 | tf_op jit(solution)/shard_map/ppermute | solution.py:19
  34.0 7.8 %collective-permute-start.3 = (bf16[40,1792]{1,0:T(8,128)(2,1)S(1)}, bf16[40,1792]{1,0:T(8,128)(2,1)S(1)}, u32[]{:S(2)}, u32[]{:S(2)}) collective-permute-start(bf16[40,1792]{1,0:T(8,128)(2,1)S(1)} %collective-permute-done.2), channel_id=1, source_target_pairs={{0,1},{1,2},{2,3},{3,4},{4,5},{5,6},{6,7},{7,0},{8,9},{9,10},{10,1... | collective-permute-start | bytes 430088 | tf_op jit(solution)/shard_map/ppermute | solution.py:19
  41.8 7.8 %collective-permute-start.4 = (bf16[40,1792]{1,0:T(8,128)(2,1)S(1)}, bf16[40,1792]{1,0:T(8,128)(2,1)S(1)}, u32[]{:S(2)}, u32[]{:S(2)}) collective-permute-start(bf16[40,1792]{1,0:T(8,128)(2,1)S(1)} %collective-permute-done.3), channel_id=1, source_target_pairs={{0,1},{1,2},{2,3},{3,4},{4,5},{5,6},{6,7},{7,0},{8,9},{9,10},{10,1... | collective-permute-start | bytes 430088 | tf_op jit(solution)/shard_map/ppermute | solution.py:19
  49.7 9.0 %collective-permute-start.5 = (bf16[40,1792]{1,0:T(8,128)(2,1)S(1)}, bf16[40,1792]{1,0:T(8,128)(2,1)S(1)}, u32[]{:S(2)}, u32[]{:S(2)}) collective-permute-start(bf16[40,1792]{1,0:T(8,128)(2,1)S(1)} %collective-permute-done.4), channel_id=1, source_target_pairs={{0,1},{1,2},{2,3},{3,4},{4,5},{5,6},{6,7},{7,0},{8,9},{9,10},{10,1... | collective-permute-start | bytes 430088 | tf_op jit(solution)/shard_map/ppermute | solution.py:19
  58.7 7.8 %collective-permute-start.6 = (bf16[40,1792]{1,0:T(8,128)(2,1)S(1)}, bf16[40,1792]{1,0:T(8,128)(2,1)S(1)}, u32[]{:S(2)}, u32[]{:S(2)}) collective-permute-start(bf16[40,1792]{1,0:T(8,128)(2,1)S(1)} %collective-permute-done.5), channel_id=1, source_target_pairs={{0,1},{1,2},{2,3},{3,4},{4,5},{5,6},{6,7},{7,0},{8,9},{9,10},{10,1... | collective-permute-start | bytes 430088 | tf_op jit(solution)/shard_map/ppermute | solution.py:19
  67.0 130.9 %copy-start.3 = (f32[1792]{0:T(1024)S(1)}, f32[1792]{0:T(1024)}, u32[]{:S(2)}) copy-start(f32[1792]{0:T(1024)} %param.13) | copy-start | bytes 21508
Sparse Core Ops, SparseCore 0:
  8.9 52.4 all-gather.2
  62.9 49.6 all-gather.4
  128.2 69.6 reduce-scatter.1
